TPU v7x, 32 devices: a whole 2x2x4 slice. The times are simulated.
32 devices in a mesh: pipe: 2 (over core), tensor: 2 (over x), expert: 8 (over z, y).
Axes of the slice: x: 2, y: 2, z: 4, core: 2. Of those that a mesh axis runs over, the one named last changes fastest.
Arguments:
- tokens: bfloat16 [3, 384, 4096], P(None, 'expert', 'tensor'), may hold values from -36 to 36
- norm_gain: float32 [2, 4096], P('pipe'), may hold values from 0.1 to 1.9
- shared_gate: bfloat16 [2, 4096, 1024], P('pipe', 'expert', 'tensor'), may hold values from -0.09375 to 0.09375
- shared_up: bfloat16 [2, 4096, 1024], P('pipe', 'expert', 'tensor'), may hold values from -0.09375 to 0.09375
- shared_down: bfloat16 [2, 1024, 4096], P('pipe', 'tensor', 'expert'), may hold values from -0.1875 to 0.1875
- expert_gate: bfloat16 [2, 8, 4096, 1024], P('pipe', 'expert', None, 'tensor'), may hold values from -0.09375 to 0.09375
- expert_up: bfloat16 [2, 8, 4096, 1024], P('pipe', 'expert', None, 'tensor'), may hold values from -0.09375 to 0.09375
- expert_down: bfloat16 [2, 8, 1024, 4096], P('pipe', 'expert', 'tensor'), may hold values from -0.1875 to 0.1875
- expert_ids: int32 [2, 3, 384, 8], P('pipe', None, 'expert'), may hold values from 0 to 255, as said below
- expert_slots: int32 [2, 3, 384, 8], P('pipe', None, 'expert'), may hold values from -1 to 2, as said below
- route_weights: float32 [2, 3, 384, 8], P('pipe', None, 'expert'), may hold values from 0.1 to 1
Outputs:
- states: bfloat16 [2, 3, 384, 4096], P('pipe', None, 'expert', 'tensor')
Inputs may be any that keep to these rules, and one draw needn't show every extreme that they name: `expert_ids`: the 8 ids of a token are distinct. Ids of 8 and above name experts that are not held and add nothing. `expert_slots`: for a choice whose id is below 8: the number of earlier choices (earlier tokens, or lower k of the same token) of the same block of 48 tokens, same layer and microbatch, that name the same expert, if that number is below 3; otherwise -1. For ids of 8 and above: -1.
All inputs are finite; a program needn't handle non-finite values.
Results may differ from a plain program's by a relative error of at most 0.0085.
Values may be sent and summed in bfloat16 or wider, within the bound.
A program may use at most 64 MiB of HBM per device.

v0:
```python
import jax
import jax.numpy as jnp
from jax import lax
from jax.sharding import PartitionSpec as P

CAP = 3


def from_behind(value, axis, steps):
    count = lax.axis_size(axis)
    initial, last = (max(0, -steps), min(count, count - steps))
    return lax.ppermute(value, axis, [(source, source + steps) for source in range(initial, last)])


def product(left, right):
    return jnp.dot(left, right, preferred_element_type=jnp.float32)


def per_device(
    tokens,
    norm_gain,
    shared_gate,
    shared_up,
    shared_down,
    expert_gate,
    expert_up,
    expert_down,
    expert_ids,
    expert_slots,
    route_weights,
):
    section_index = lax.axis_index("pipe")
    n_experts = lax.axis_size("expert")
    n_tensor = lax.axis_size("tensor")
    batches = tokens.shape[0]
    shard_rows = tokens.shape[1]
    slice_width = tokens.shape[2]
    model_width = slice_width * n_tensor
    capacity = CAP
    slot_total = n_experts * capacity
    slot_range = jnp.arange(slot_total, dtype=jnp.int32)
    shared_gate_full, shared_up_full, shared_down_full = (
        lax.all_gather(shared_gate[0], "expert", axis=0, tiled=True),
        lax.all_gather(shared_up[0], "expert", axis=0, tiled=True),
        lax.all_gather(shared_down[0], "expert", axis=1, tiled=True),
    )
    local_gate = expert_gate[0, 0]
    local_up = expert_up[0, 0]
    local_down = expert_down[0, 0]
    layer_gain = norm_gain[0]
    incoming = jnp.zeros((shard_rows, slice_width), jnp.bfloat16)
    produced = []
    for step_index in range(batches + 1):
        fresh_rows = tokens[min(step_index, batches - 1)]
        current = jnp.where(section_index == 0, fresh_rows, incoming)
        batch_index = jnp.clip(step_index - section_index, 0, batches - 1)
        route_ids = lax.dynamic_index_in_dim(expert_ids[0], batch_index, 0, keepdims=False)
        slot_rank = lax.dynamic_index_in_dim(expert_slots[0], batch_index, 0, keepdims=False)
        weights = lax.dynamic_index_in_dim(route_weights[0], batch_index, 0, keepdims=False)
        full_rows = lax.all_gather(current, "tensor", axis=1, tiled=True)
        values = full_rows.astype(jnp.float32)
        inverse_rms = lax.rsqrt(jnp.mean(values * values, axis=-1, keepdims=True) + 1e-06)
        normed = (values * inverse_rms * layer_gain).astype(jnp.bfloat16)
        shared_hidden = (
            jax.nn.silu(product(normed, shared_gate_full)) * product(normed, shared_up_full)
        ).astype(jnp.bfloat16)
        partial_value = product(shared_hidden, shared_down_full)
        valid = (route_ids < n_experts) & (slot_rank >= 0)
        slot_code = jnp.where(valid, route_ids * capacity + slot_rank, -1)
        matched = slot_code[:, :, None] == slot_range[None, None, :]
        picker = jnp.any(matched, axis=1).T.astype(jnp.bfloat16)
        combine = jnp.sum(jnp.where(matched, weights[:, :, None], jnp.float32(0.0)), axis=1)
        outgoing = (
            product(picker, normed).astype(jnp.bfloat16).reshape(n_experts, capacity, model_width)
        )
        arrived = lax.all_to_all(
            outgoing, "expert", split_axis=0, concat_axis=0, tiled=True
        ).reshape(slot_total, model_width)
        gate_rows = product(arrived, local_gate)
        up_rows = product(arrived, local_up)
        expert_hidden = (jax.nn.silu(gate_rows) * up_rows).astype(jnp.bfloat16)
        outcome = (
            product(expert_hidden, local_down)
            .astype(jnp.bfloat16)
            .reshape(n_experts, capacity, model_width)
        )
        returned = lax.all_to_all(
            outcome, "expert", split_axis=0, concat_axis=0, tiled=True
        ).reshape(slot_total, model_width)
        routed = jnp.dot(
            combine,
            returned.astype(jnp.float32),
            precision=lax.Precision.HIGHEST,
            preferred_element_type=jnp.float32,
        )
        summed = lax.psum_scatter(
            (partial_value + routed).astype(jnp.bfloat16), "tensor", scatter_dimension=1, tiled=True
        ).astype(jnp.float32)
        result = (current.astype(jnp.float32) + summed).astype(jnp.bfloat16)
        produced.append(result)
        if step_index < batches:
            incoming = from_behind(result, "pipe", 1)
    outputs = [
        jnp.where(section_index == 0, produced[index_now], produced[index_now + 1])
        for index_now in range(batches)
    ]
    return jnp.stack(outputs)[None]


def solution(mesh):
    in_specs = (
        P(None, "expert", "tensor"),
        P("pipe", None),
        P("pipe", "expert", "tensor"),
        P("pipe", "expert", "tensor"),
        P("pipe", "tensor", "expert"),
        P("pipe", "expert", None, "tensor"),
        P("pipe", "expert", None, "tensor"),
        P("pipe", "expert", "tensor", None),
        P("pipe", None, "expert", None),
        P("pipe", None, "expert", None),
        P("pipe", None, "expert", None),
    )
    out_specs = P("pipe", None, "expert", "tensor")
    return jax.shard_map(
        per_device, mesh=mesh, in_specs=in_specs, out_specs=out_specs, check_vma=False
    )
```

profile of v0, /device:TPU:13, one launch (start us, length us, event | category | flops | bytes accessed | tf_op | source)
XLA Modules:
  0.0 462.3 jit_solution(17845776219096333641)
XLA Ops:
  9.7 6.4 %all-gather = bf16[1,48,4096]{2,1,0:T(8,128)(2,1)S(1)} all-gather(bf16[1,48,2048]{2,1,0:T(8,128)(2,1)S(1)} %slice_select_fusion), channel_id=2, replica_groups=mesh['pipe'=2,'tensor'=2,'expert'=8] {'tensor'}, dimensions={2}, use_global_device_ids=true | all-gather | bytes 589824 | tf_op jit(solution)/shard_map/all_gather | solution.py:60
  18.3 18.1 %all_to_all.40 = bf16[8,3,4096]{2,1,0:T(4,128)(2,1)S(1)} all-to-all(bf16[8,3,4096]{2,1,0:T(4,128)(2,1)S(1)} %reshape.235), channel_id=1, replica_groups=mesh['pipe'=2,'tensor'=2,'expert'=8] {'expert'}, dimensions={0} | all-to-all | bytes 393216 | tf_op jit(solution)/shard_map/all_to_all | solution.py:76
  39.4 4.8 %convolution_convert_fusion.6 = bf16[24,4096]{1,0:T(8,128)(2,1)S(1)} fusion(bf16[1,1,512,4096]{3,2,1,0:T(8,128)(2,1)} %param.18, bf16[24,4096]{1,0:T(8,128)(2,1)S(1)} %reshape.236, bf16[1,1,4096,512]{3,2,1,0:T(8,128)(2,1)} %param.17, f32[24,512]{1,0:T(8,128)S(1)} %fusion.22), kind=kOutput, calls=%fused_computation.14 | convolution fusion | flops 201498624 | bytes 8830976 | tf_op jit(solution)/shard_map/dot_general | solution.py:16
  45.1 7.1 %all-to-all-start.1 = ((bf16[8,3,4096]{2,1,0:T(4,128)(2,1)}), bf16[8,3,4096]{2,1,0:T(4,128)(2,1)S(1)}, u32[]{:S(2)}, u32[]{:S(2)}) async-start(bf16[8,3,4096]{2,1,0:T(4,128)(2,1)} %reshape.237), calls=%async_computation.1 | async-start | bytes 524288 | tf_op jit(solution)/shard_map/all_to_all | solution.py:87
  52.2 12.7 %all-to-all-done.1 = bf16[8,3,4096]{2,1,0:T(4,128)(2,1)S(1)} async-done(((bf16[8,3,4096]{2,1,0:T(4,128)(2,1)}), bf16[8,3,4096]{2,1,0:T(4,128)(2,1)S(1)}, u32[]{:S(2)}, u32[]{:S(2)}) %all-to-all-start.1) | async-done | bytes 196640 | tf_op jit(solution)/shard_map/all_to_all | solution.py:87
  65.7 23.9 %all-gather.8.cloned.1.call-done = bf16[1,4096,512]{2,1,0:T(8,128)(2,1)} async-done(((bf16[1,512,512]{2,1,0:T(8,128)(2,1)}), bf16[1,4096,512]{2,1,0:T(8,128)(2,1)}) %all-gather.8.cloned.1.call-update) | async-done | bytes 4194320 | tf_op jit(solution)/shard_map/all_gather | solution.py:43
  89.5 3.1 fusion.42
  92.6 70.9 %all-gather.10.cloned.1.call-done = bf16[1,4096,512]{2,1,0:T(8,128)(2,1)} async-done(((bf16[1,512,512]{2,1,0:T(8,128)(2,1)}), bf16[1,4096,512]{2,1,0:T(8,128)(2,1)}) %all-gather.10.cloned.1.call-update) | async-done | bytes 4194320 | tf_op jit(solution)/shard_map/all_gather | solution.py:44
  163.6 74.9 %all-gather.12.cloned.1.call-done = bf16[1,512,4096]{2,1,0:T(8,128)(2,1)} async-done(((bf16[1,512,512]{2,1,0:T(8,128)(2,1)}), bf16[1,512,4096]{2,1,0:T(8,128)(2,1)}) %all-gather.12.cloned.1.call-update) | async-done | bytes 4194320 | tf_op jit(solution)/shard_map/all_gather | solution.py:45
  238.5 5.9 %fusion = bf16[48,4096]{1,0:T(8,128)(2,1)} fusion(f32[48,4096]{1,0:T(8,128)S(1)} %fusion.199, bf16[1,512,4096]{2,1,0:T(8,128)(2,1)} %all-gather.12.cloned.1.call-done, bf16[1,4096,512]{2,1,0:T(8,128)(2,1)} %all-gather.10.cloned.1.call-done, f32[48,512]{1,0:T(8,128)S(1)} %fusion.42, bf16[1,48,4096]{2,1,0:T(8,128)(2,1)S(1)} %all-gather, ...), kind=kOutput, calls=%fused_computation.4 | convolution fusion | flops 403980288 | bytes 10076352 | tf_op jit(solution)/shard_map/dot_general | solution.py:16
  244.4 14.7 %reduce-scatter.5.cloned.1.call-done = bf16[48,2048]{1,0:T(8,128)(2,1)} async-done(((bf16[48,4096]{1,0:T(8,128)(2,1)}), bf16[48,2048]{1,0:T(8,128)(2,1)}) %reduce-scatter.5.cloned.1.call-update) | async-done | bytes 196624 | tf_op jit(solution)/shard_map/reduce_scatter | solution.py:96
  263.4 7.0 %all_gather.25 = bf16[48,4096]{1,0:T(8,128)(2,1)S(1)} all-gather(bf16[48,2048]{1,0:T(8,128)(2,1)S(1)} %bitcast_select_fusion.2), channel_id=1, replica_groups=mesh['pipe'=2,'tensor'=2,'expert'=8] {'tensor'}, dimensions={1}, use_global_device_ids=true | all-gather | bytes 589824 | tf_op jit(solution)/shard_map/all_gather | solution.py:60
  271.0 11.0 %all_to_all.41 = bf16[8,3,4096]{2,1,0:T(4,128)(2,1)S(1)} all-to-all(bf16[8,3,4096]{2,1,0:T(4,128)(2,1)S(1)} %reshape.239), channel_id=1, replica_groups=mesh['pipe'=2,'tensor'=2,'expert'=8] {'expert'}, dimensions={0} | all-to-all | bytes 393216 | tf_op jit(solution)/shard_map/all_to_all | solution.py:76
  285.1 4.8 %convolution_convert_fusion.4 = bf16[24,4096]{1,0:T(8,128)(2,1)S(1)} fusion(bf16[1,1,512,4096]{3,2,1,0:T(8,128)(2,1)} %param.18, bf16[24,4096]{1,0:T(8,128)(2,1)S(1)} %reshape.240, bf16[1,1,4096,512]{3,2,1,0:T(8,128)(2,1)} %param.17, f32[24,512]{1,0:T(8,128)S(1)} %fusion.20), kind=kOutput, calls=%fused_computation.12 | convolution fusion | flops 201498624 | bytes 8830976 | tf_op jit(solution)/shard_map/dot_general | solution.py:16
  290.7 6.3 %all-to-all-start.3 = ((bf16[8,3,4096]{2,1,0:T(4,128)(2,1)}), bf16[8,3,4096]{2,1,0:T(4,128)(2,1)S(1)}, u32[]{:S(2)}, u32[]{:S(2)}) async-start(bf16[8,3,4096]{2,1,0:T(4,128)(2,1)} %reshape.241), calls=%async_computation.4 | async-start | bytes 524288 | tf_op jit(solution)/shard_map/all_to_all | solution.py:87
  297.1 3.1 fusion.40
  303.5 5.9 %fusion.1 = bf16[48,4096]{1,0:T(8,128)(2,1)} fusion(f32[48,4096]{1,0:T(8,128)S(1)} %fusion.200, bf16[1,512,4096]{2,1,0:T(8,128)(2,1)} %all-gather.12.cloned.1.call-done, bf16[1,4096,512]{2,1,0:T(8,128)(2,1)} %all-gather.10.cloned.1.call-done, f32[48,512]{1,0:T(8,128)S(1)} %fusion.40, bf16[48,4096]{1,0:T(8,128)(2,1)S(1)} %all_gather.25, ...), kind=kOutput, calls=%fused_computation.5 | convolution fusion | flops 403980288 | bytes 10076352 | tf_op jit(solution)/shard_map/dot_general | solution.py:16
  309.4 14.4 %reduce-scatter.7.cloned.1.call-done = bf16[48,2048]{1,0:T(8,128)(2,1)} async-done(((bf16[48,4096]{1,0:T(8,128)(2,1)}), bf16[48,2048]{1,0:T(8,128)(2,1)}) %reduce-scatter.7.cloned.1.call-update) | async-done | bytes 196624 | tf_op jit(solution)/shard_map/reduce_scatter | solution.py:96
  328.3 7.0 %all_gather.26 = bf16[48,4096]{1,0:T(8,128)(2,1)S(1)} all-gather(bf16[48,2048]{1,0:T(8,128)(2,1)S(1)} %bitcast_select_fusion.1), channel_id=1, replica_groups=mesh['pipe'=2,'tensor'=2,'expert'=8] {'tensor'}, dimensions={1}, use_global_device_ids=true | all-gather | bytes 589824 | tf_op jit(solution)/shard_map/all_gather | solution.py:60
  335.9 11.0 %all_to_all.42 = bf16[8,3,4096]{2,1,0:T(4,128)(2,1)S(1)} all-to-all(bf16[8,3,4096]{2,1,0:T(4,128)(2,1)S(1)} %reshape.243), channel_id=1, replica_groups=mesh['pipe'=2,'tensor'=2,'expert'=8] {'expert'}, dimensions={0} | all-to-all | bytes 393216 | tf_op jit(solution)/shard_map/all_to_all | solution.py:76
  349.9 4.8 %convolution_convert_fusion.2 = bf16[24,4096]{1,0:T(8,128)(2,1)S(1)} fusion(bf16[1,1,512,4096]{3,2,1,0:T(8,128)(2,1)} %param.18, bf16[24,4096]{1,0:T(8,128)(2,1)S(1)} %reshape.244, bf16[1,1,4096,512]{3,2,1,0:T(8,128)(2,1)} %param.17, f32[24,512]{1,0:T(8,128)S(1)} %fusion.18), kind=kOutput, calls=%fused_computation.10 | convolution fusion | flops 201498624 | bytes 8830976 | tf_op jit(solution)/shard_map/dot_general | solution.py:16
  355.6 6.3 %all-to-all-start.5 = ((bf16[8,3,4096]{2,1,0:T(4,128)(2,1)}), bf16[8,3,4096]{2,1,0:T(4,128)(2,1)S(1)}, u32[]{:S(2)}, u32[]{:S(2)}) async-start(bf16[8,3,4096]{2,1,0:T(4,128)(2,1)} %reshape.245), calls=%async_computation.7 | async-start | bytes 524288 | tf_op jit(solution)/shard_map/all_to_all | solution.py:87
  361.9 3.1 fusion.38
  368.4 5.9 %fusion.2 = bf16[48,4096]{1,0:T(8,128)(2,1)} fusion(f32[48,4096]{1,0:T(8,128)S(1)} %fusion.201, bf16[1,512,4096]{2,1,0:T(8,128)(2,1)} %all-gather.12.cloned.1.call-done, bf16[1,4096,512]{2,1,0:T(8,128)(2,1)} %all-gather.10.cloned.1.call-done, f32[48,512]{1,0:T(8,128)S(1)} %fusion.38, bf16[48,4096]{1,0:T(8,128)(2,1)S(1)} %all_gather.26, ...), kind=kOutput, calls=%fused_computation.6 | convolution fusion | flops 403980288 | bytes 10076352 | tf_op jit(solution)/shard_map/dot_general | solution.py:16
  374.3 14.4 %reduce-scatter.9.cloned.1.call-done = bf16[48,2048]{1,0:T(8,128)(2,1)} async-done(((bf16[48,4096]{1,0:T(8,128)(2,1)}), bf16[48,2048]{1,0:T(8,128)(2,1)}) %reduce-scatter.9.cloned.1.call-update) | async-done | bytes 196624 | tf_op jit(solution)/shard_map/reduce_scatter | solution.py:96
  393.1 7.0 %all_gather.27 = bf16[48,4096]{1,0:T(8,128)(2,1)S(1)} all-gather(bf16[48,2048]{1,0:T(8,128)(2,1)S(1)} %bitcast_select_fusion), channel_id=1, replica_groups=mesh['pipe'=2,'tensor'=2,'expert'=8] {'tensor'}, dimensions={1}, use_global_device_ids=true | all-gather | bytes 589824 | tf_op jit(solution)/shard_map/all_gather | solution.py:60
  400.7 11.0 %all_to_all.43 = bf16[8,3,4096]{2,1,0:T(4,128)(2,1)S(1)} all-to-all(bf16[8,3,4096]{2,1,0:T(4,128)(2,1)S(1)} %reshape.247), channel_id=1, replica_groups=mesh['pipe'=2,'tensor'=2,'expert'=8] {'expert'}, dimensions={0} | all-to-all | bytes 393216 | tf_op jit(solution)/shard_map/all_to_all | solution.py:76
  414.8 4.8 %convolution_convert_fusion = bf16[24,4096]{1,0:T(8,128)(2,1)S(1)} fusion(bf16[1,1,512,4096]{3,2,1,0:T(8,128)(2,1)} %param.18, bf16[24,4096]{1,0:T(8,128)(2,1)S(1)} %reshape.248, bf16[1,1,4096,512]{3,2,1,0:T(8,128)(2,1)} %param.17, f32[24,512]{1,0:T(8,128)S(1)} %fusion.16), kind=kOutput, calls=%fused_computation.8 | convolution fusion | flops 201498624 | bytes 8830976 | tf_op jit(solution)/shard_map/dot_general | solution.py:16
  420.4 6.3 %all-to-all-start.7 = ((bf16[8,3,4096]{2,1,0:T(4,128)(2,1)}), bf16[8,3,4096]{2,1,0:T(4,128)(2,1)S(1)}, u32[]{:S(2)}, u32[]{:S(2)}) async-start(bf16[8,3,4096]{2,1,0:T(4,128)(2,1)} %reshape.249), calls=%async_computation.10 | async-start | bytes 524288 | tf_op jit(solution)/shard_map/all_to_all | solution.py:87
  426.8 3.1 fusion.36
  433.3 5.9 %fusion.3 = bf16[48,4096]{1,0:T(8,128)(2,1)} fusion(f32[48,4096]{1,0:T(8,128)S(1)} %fusion.202, bf16[1,512,4096]{2,1,0:T(8,128)(2,1)} %all-gather.12.cloned.1.call-done, bf16[1,4096,512]{2,1,0:T(8,128)(2,1)} %all-gather.10.cloned.1.call-done, f32[48,512]{1,0:T(8,128)S(1)} %fusion.36, bf16[48,4096]{1,0:T(8,128)(2,1)S(1)} %all_gather.27, ...), kind=kOutput, calls=%fused_computation.7 | convolution fusion | flops 403980288 | bytes 10076352 | tf_op jit(solution)/shard_map/dot_general | solution.py:16
  439.2 14.4 %reduce-scatter.11.cloned.1.call-done = bf16[48,2048]{1,0:T(8,128)(2,1)} async-done(((bf16[48,4096]{1,0:T(8,128)(2,1)}), bf16[48,2048]{1,0:T(8,128)(2,1)}) %reduce-scatter.11.cloned.1.call-update) | async-done | bytes 196624 | tf_op jit(solution)/shard_map/reduce_scatter | solution.py:96
  (84 shorter events, 48.5 us)
Async XLA Ops:
  6.5 83.0 %all-gather.8.cloned.1.call-start = ((), (), s32[]{:S(2)}) async-start(), calls=%async_computation.16 | async-start | bytes 4718592 | tf_op jit(solution)/shard_map/all_gather | solution.py:43
  7.3 156.3 %all-gather.10.cloned.1.call-start = ((), (), s32[]{:S(2)}) async-start(), calls=%async_computation.17 | async-start | bytes 4718592 | tf_op jit(solution)/shard_map/all_gather | solution.py:44
  8.0 230.5 %all-gather.12.cloned.1.call-start = ((), (), s32[]{:S(2)}) async-start(), calls=%async_computation.18 | async-start | bytes 4718592 | tf_op jit(solution)/shard_map/all_gather | solution.py:45
  39.4 12.7 %copy-start.2 = (f32[1,3,48,8]{2,3,1,0:T(8,128)S(1)}, f32[1,3,48,8]{2,3,1,0:T(8,128)}, u32[]{:S(2)}) copy-start(f32[1,3,48,8]{2,3,1,0:T(8,128)} %param.21) | copy-start | bytes 13828
  39.4 50.1 %copy-start.1 = (f32[1,4096]{1,0:T(1,128)S(1)}, f32[1,4096]{1,0:T(1,128)}, u32[]{:S(2)}) copy-start(f32[1,4096]{1,0:T(1,128)} %param.12) | copy-start | bytes 49156
  45.1 19.9 %all-to-all-start.1 = ((bf16[8,3,4096]{2,1,0:T(4,128)(2,1)}), bf16[8,3,4096]{2,1,0:T(4,128)(2,1)S(1)}, u32[]{:S(2)}, u32[]{:S(2)}) async-start(bf16[8,3,4096]{2,1,0:T(4,128)(2,1)} %reshape.237), calls=%async_computation.1 | async-start | bytes 524288 | tf_op jit(solution)/shard_map/all_to_all | solution.py:87
  52.2 206.9 %reduce-scatter.5.cloned.1.call-start = ((), (), s32[]{:S(2)}) async-start(), calls=%async_computation.12 | async-start | bytes 589824 | tf_op jit(solution)/shard_map/reduce_scatter | solution.py:96
  92.6 166.4 %copy-start = (bf16[3,48,2048]{2,1,0:T(8,128)(2,1)S(1)}, bf16[3,48,2048]{2,1,0:T(8,128)(2,1)}, u32[]{:S(2)}) copy-start(bf16[3,48,2048]{2,1,0:T(8,128)(2,1)} %param.11) | copy-start | bytes 1769476
  260.0 3.3 collective-permute-start
  290.7 12.1 %all-to-all-start.3 = ((bf16[8,3,4096]{2,1,0:T(4,128)(2,1)}), bf16[8,3,4096]{2,1,0:T(4,128)(2,1)S(1)}, u32[]{:S(2)}, u32[]{:S(2)}) async-start(bf16[8,3,4096]{2,1,0:T(4,128)(2,1)} %reshape.241), calls=%async_computation.4 | async-start | bytes 524288 | tf_op jit(solution)/shard_map/all_to_all | solution.py:87
  297.0 26.8 %reduce-scatter.7.cloned.1.call-start = ((), (), s32[]{:S(2)}) async-start(), calls=%async_computation.13 | async-start | bytes 589824 | tf_op jit(solution)/shard_map/reduce_scatter | solution.py:96
  324.9 3.3 collective-permute-start.1
  355.6 12.1 %all-to-all-start.5 = ((bf16[8,3,4096]{2,1,0:T(4,128)(2,1)}), bf16[8,3,4096]{2,1,0:T(4,128)(2,1)S(1)}, u32[]{:S(2)}, u32[]{:S(2)}) async-start(bf16[8,3,4096]{2,1,0:T(4,128)(2,1)} %reshape.245), calls=%async_computation.7 | async-start | bytes 524288 | tf_op jit(solution)/shard_map/all_to_all | solution.py:87
  361.9 26.8 %reduce-scatter.9.cloned.1.call-start = ((), (), s32[]{:S(2)}) async-start(), calls=%async_computation.14 | async-start | bytes 589824 | tf_op jit(solution)/shard_map/reduce_scatter | solution.py:96
  389.8 3.3 collective-permute-start.2
  420.4 12.1 %all-to-all-start.7 = ((bf16[8,3,4096]{2,1,0:T(4,128)(2,1)}), bf16[8,3,4096]{2,1,0:T(4,128)(2,1)S(1)}, u32[]{:S(2)}, u32[]{:S(2)}) async-start(bf16[8,3,4096]{2,1,0:T(4,128)(2,1)} %reshape.249), calls=%async_computation.10 | async-start | bytes 524288 | tf_op jit(solution)/shard_map/all_to_all | solution.py:87
  426.8 26.8 %reduce-scatter.11.cloned.1.call-start = ((), (), s32[]{:S(2)}) async-start(), calls=%async_computation.15 | async-start | bytes 589824 | tf_op jit(solution)/shard_map/reduce_scatter | solution.py:96
Sparse Core Ops, SparseCore 0:
  9.5 80.0 all-gather.7
  91.7 71.8 all-gather.9
  165.6 72.8 all-gather.11
  244.5 14.4 reduce-scatter.4
  309.6 14.2 reduce-scatter.6
  374.4 14.2 reduce-scatter.8
  439.3 14.2 reduce-scatter.10
where the time goes:
time: 465 us; the launch traced here: 462 us
  waiting for transfers between devices  257 us (55%)
  blocking collectives  78.6 us (17%)
  matrix products  70.4 us (15%)
  starting transfers between devices  30.1 us (6%)
  between operations  13.7 us (3%)
  other arithmetic  7.68 us (2%)
  local copies, waits for them, and re-layouts  5.27 us (1%)
    all_gather x1, waiting for transfers between devices, per_device(): lax.all_gather(shared_down[0], 'expert', axis=1, tiled=True)  74.9 us
    all_gather x1, waiting for transfers between devices, per_device(): lax.all_gather(shared_up[0], 'expert', axis=0, tiled=True)  70.9 us
    dot_general x20, matrix products, product(): return jnp.dot(left, right, preferred_element_type=jnp.float32)  68.3 us
    reduce_scatter x4, waiting for transfers between devices, per_device(): lax.psum_scatter((partial_value + routed).astype(jnp.bfloat16), 'tensor',...  57.9 us
    all_to_all x4, blocking collectives, per_device(): lax.all_to_all(outgoing, 'expert', split_axis=0, concat_axis=0, tiled=True)  51.2 us
    all_gather x4, blocking collectives, per_device(): full_rows = lax.all_gather(current, 'tensor', axis=1, tiled=True)  27.4 us
    all_to_all x4, starting transfers between devices, per_device(): lax.all_to_all(outcome, 'expert', split_axis=0, concat_axis=0, tiled=True)  26.1 us
    all_gather x1, waiting for transfers between devices, per_device(): lax.all_gather(shared_gate[0], 'expert', axis=0, tiled=True)  23.9 us
  transfers between devices with their start and end apart: 14, of which 14 were waited for; matrix products, arithmetic and copies ran while one was open for 5% of the time, Pallas kernels for 0%

commit v1 on v0

v1 whole, which is shorter than its diff:
```python
import functools

import jax
import jax.numpy as jnp
from jax import lax
from jax.experimental import pallas as pl
from jax.experimental.pallas import tpu as pltpu
from jax.sharding import PartitionSpec as P

CAP = 3
MESH = pl.DeviceIdType.MESH
F32 = jnp.float32
BF16 = jnp.bfloat16


def product(left, right):
    return jnp.dot(left, right, preferred_element_type=F32)


def silu(value):
    return value / (1.0 + jnp.exp(-value))


def layer_kernel(
    ne, nt,
    x_hbm, gain, picker, combine, sg_hbm, su_hbm, sd_hbm, eg_hbm, eu_hbm, ed_hbm,
    out,
    xs, xn, sg, su, sd, eg, eu, ed,
    outg, arr, outc, ret, g_acc, u_acc, hid, eg_acc, eu_acc, ehid, y, rs, res,
    w_send, w_recv, d_send, d_recv, x_send, x_recv, a_send, a_recv, b_send, b_recv,
    r_send, r_recv, p_send, p_recv, own_sem, exp_sem, x_sem, go_sem,
):
    pipe = lax.axis_index("pipe")
    ten = lax.axis_index("tensor")
    me = lax.axis_index("expert")
    spt = ne // nt
    T, Ds = xs.shape[1], xs.shape[2]
    F = sg.shape[2]
    rows = outg.shape[1]
    half = F // 2
    base = ten * spt

    odd = me % 2
    pos = (1 - odd) * (me // 2) + odd * (ne - 1 - me // 2)

    def at(p):
        p = (p + 2 * ne) % ne
        upper = p // (ne // 2)
        return (1 - upper) * (2 * p) + upper * (2 * (ne - 1 - p) + 1)

    def remote(src, dst, send, recv, **device):
        return pltpu.make_async_remote_copy(
            src_ref=src, dst_ref=dst, send_sem=send, recv_sem=recv,
            device_id=device, device_id_type=MESH,
        )

    barrier = pltpu.get_barrier_semaphore()
    for k in range(1, ne):
        pl.semaphore_signal(barrier, inc=1, device_id={"expert": (me + k) % ne}, device_id_type=MESH)
    for k in range(1, nt):
        pl.semaphore_signal(barrier, inc=1, device_id={"tensor": (ten + k) % nt}, device_id_type=MESH)
    pl.semaphore_signal(barrier, inc=1, device_id={"pipe": 1 - pipe}, device_id_type=MESH)

    own = [
        pltpu.make_async_copy(sg_hbm, sg.at[me], own_sem.at[0]),
        pltpu.make_async_copy(su_hbm, su.at[me], own_sem.at[1]),
        pltpu.make_async_copy(sd_hbm, sd.at[me], own_sem.at[2]),
    ]
    for copy in own:
        copy.start()
    x_in = [
        pltpu.make_async_copy(x_hbm.at[:, pl.ds(i * Ds, Ds)], xs.at[base + i], x_sem.at[i])
        for i in range(spt)
    ]

    @pl.when(pipe == 0)
    def _():
        for copy in x_in:
            copy.start()

    experts = [
        pltpu.make_async_copy(eg_hbm, eg, exp_sem.at[0]),
        pltpu.make_async_copy(eu_hbm, eu, exp_sem.at[1]),
        pltpu.make_async_copy(ed_hbm, ed, exp_sem.at[2]),
    ]
    for copy in experts:
        copy.start()
    pl.semaphore_wait(barrier, ne - 1 + nt - 1 + 1)

    right, left = at(pos + 1), at(pos - 1)

    def gate_copy(s):
        block = sg.at[at(pos - s)]
        return remote(block, block, w_send.at[0, s], w_recv.at[0, s], expert=right)

    def up_copy(s):
        block = su.at[at(pos + s)]
        return remote(block, block, w_send.at[1, s], w_recv.at[1, s], expert=left)

    def down_a(s):
        block = sd.at[at(pos - s), pl.ds(0, half)]
        return remote(block, block, d_send.at[0, s], d_recv.at[0, s], expert=right)

    def down_b(s):
        block = sd.at[at(pos + s), pl.ds(half, half)]
        return remote(block, block, d_send.at[1, s], d_recv.at[1, s], expert=left)

    def ring(s):
        for group in ((gate_copy, up_copy), (down_a, down_b)):
            for make in group:
                make(s).wait_recv()
                if s + 1 < ne - 1:
                    make(s + 1).start()

    @pl.when(pipe == 1)
    def _():
        pl.semaphore_wait(go_sem, 1)

    for copy in own:
        copy.wait()
    for make in (gate_copy, up_copy, down_a, down_b):
        make(0).start()

    @pl.when(pipe == 0)
    def _():
        for copy in x_in:
            copy.wait()

    @pl.when(pipe == 1)
    def _():
        for i in range(spt):
            block = xs.at[base + i]
            remote(block, block, p_send.at[i], p_recv.at[i], pipe=1 - pipe).wait_recv()

    def x_copy(k, i):
        block = xs.at[base + i]
        return remote(block, block, x_send.at[k - 1, i], x_recv.at[k - 1, i], tensor=(ten + k) % nt)

    for k in range(1, nt):
        for i in range(spt):
            x_copy(k, i).start()
    ring(0)
    for k in range(1, nt):
        for i in range(spt):
            x_copy(k, i).wait_recv()

    def squares(j, total):
        v = xs[j].astype(F32)
        return total + jnp.sum(v * v, axis=-1, keepdims=True)

    total = lax.fori_loop(0, ne, squares, jnp.zeros((T, 1), F32))
    inverse = lax.rsqrt(total / (ne * Ds) + 1e-06)

    def normalise(j, carry):
        v = (xs[j].astype(F32) * inverse * gain[j]).astype(BF16)
        xn[j] = v
        sent = product(picker[...], v).astype(BF16).reshape(ne, rows, Ds)
        outg[:, :, pl.ds(pl.multiple_of(j * Ds, 128), Ds)] = sent
        return carry

    lax.fori_loop(0, ne, normalise, 0)

    def dispatch(k):
        to = (me + k) % ne
        return remote(outg.at[to], arr.at[me], a_send.at[k - 1], a_recv.at[k - 1], expert=to)

    def give_back(k):
        to = (me + k) % ne
        return remote(outc.at[to], ret.at[me], b_send.at[k - 1], b_recv.at[k - 1], expert=to)

    for k in range(1, ne):
        dispatch(k).start()
    arr[me] = outg[me]

    g_acc[...] = product(xn[me], sg[me])
    u_acc[...] = product(xn[me], su[me])

    def shared(s):
        a, b = at(pos - s - 1), at(pos + s + 1)
        g_acc[...] += product(xn[a], sg[a])
        u_acc[...] += product(xn[b], su[b])

    ring(1)
    ring(2)
    for copy in experts:
        copy.wait()
    for k in range(1, ne):
        dispatch(k).wait_recv()
    eg_acc[...] = jnp.zeros_like(eg_acc)
    eu_acc[...] = jnp.zeros_like(eu_acc)

    def expert_in(j, carry):
        depth = pl.ds(pl.multiple_of(j * Ds, 128), Ds)
        v = arr[:, :, depth].reshape(ne * rows, Ds)
        eg_acc[...] += product(v, eg[depth, :])
        eu_acc[...] += product(v, eu[depth, :])
        return carry

    lax.fori_loop(0, ne // 2, expert_in, 0)
    ring(3)
    lax.fori_loop(ne // 2, ne, expert_in, 0)
    ehid[...] = (silu(eg_acc[...]) * eu_acc[...]).astype(BF16)

    def expert_out(j, carry):
        width = pl.ds(pl.multiple_of(j * Ds, 128), Ds)
        outc[:, :, width] = product(ehid[...], ed[:, width]).astype(BF16).reshape(ne, rows, Ds)
        return carry

    lax.fori_loop(0, ne, expert_out, 0)
    for k in range(1, ne):
        give_back(k).start()
    ret[me] = outc[me]
    for s in range(4, ne - 1):
        ring(s)
        if s < ne - 2:
            if s == 4:
                for q in range(4):
                    shared(q)
            shared(s)

    @pl.when(pipe == 0)
    def _():
        pl.semaphore_signal(go_sem, inc=1, device_id={"pipe": 1 - pipe}, device_id_type=MESH)

    shared(ne - 2)
    hid[...] = (silu(g_acc[...]) * u_acc[...]).astype(BF16)
    for k in range(1, ne):
        give_back(k).wait_recv()
    weights = combine[...]
    high = weights.astype(BF16)
    low = (weights - high.astype(F32)).astype(BF16)

    def terms(j):
        v = ret[:, :, pl.ds(pl.multiple_of(j * Ds, 128), Ds)].reshape(ne * rows, Ds)
        return product(hid[...], sd[j]) + (product(high, v) + product(low, v))

    def r_copy(k, i):
        to = (ten + k) % nt
        slot = (k - 1) * spt + i
        return remote(y.at[slot], rs.at[slot], r_send.at[slot], r_recv.at[slot], tensor=to)

    for k in range(1, nt):
        for i in range(spt):
            y[(k - 1) * spt + i] = terms(((ten + k) % nt) * spt + i).astype(BF16)
            r_copy(k, i).start()

    for i in range(spt):
        value = xs[base + i].astype(F32) + terms(base + i)
        for k in range(1, nt):
            r_copy(k, i).wait_recv()
            value += rs[(k - 1) * spt + i].astype(F32)
        value = value.astype(BF16)
        res[i] = value
        out[:, i * Ds:(i + 1) * Ds] = value

        @pl.when(pipe == 0)
        def _():
            remote(res.at[i], xs.at[base + i], p_send.at[i], p_recv.at[i], pipe=1 - pipe).start()

    for s in range(ne - 1):
        for make in (gate_copy, up_copy, down_a, down_b):
            make(s).wait_send()
    for k in range(1, ne):
        dispatch(k).wait_send()
        give_back(k).wait_send()
    for k in range(1, nt):
        for i in range(spt):
            x_copy(k, i).wait_send()
            r_copy(k, i).wait_send()

    @pl.when(pipe == 0)
    def _():
        for i in range(spt):
            remote(res.at[i], xs.at[base + i], p_send.at[i], p_recv.at[i], pipe=1 - pipe).wait_send()


def per_device(
    tokens, norm_gain, shared_gate, shared_up, shared_down,
    expert_gate, expert_up, expert_down, expert_ids, expert_slots, route_weights,
):
    ne = lax.axis_size("expert")
    nt = lax.axis_size("tensor")
    batches, block, width = tokens.shape
    T = batches * block
    D = width * nt
    Ds = shared_gate.shape[1]
    F = shared_gate.shape[2]
    FE = expert_gate.shape[3]
    spt = ne // nt
    rows = -(-batches * CAP // 16) * 16

    ids, slots, weights = expert_ids[0], expert_slots[0], route_weights[0]
    valid = (ids < ne) & (slots >= 0)
    batch = jnp.arange(batches, dtype=jnp.int32)[:, None, None]
    code = jnp.where(valid, ids * rows + batch * CAP + slots, -1).reshape(T, -1)
    matched = code[:, :, None] == jnp.arange(ne * rows, dtype=jnp.int32)[None, None, :]
    picker = jnp.any(matched, axis=1).T.astype(BF16)
    combine = jnp.sum(jnp.where(matched, weights.reshape(T, -1)[:, :, None], F32(0.0)), axis=1)

    vmem = pl.BlockSpec(memory_space=pltpu.VMEM)
    hbm = pl.BlockSpec(memory_space=pl.ANY)
    dma = pltpu.SemaphoreType.DMA
    steps = ne - 1
    others = max(nt - 1, 1)
    out = pl.pallas_call(
        functools.partial(layer_kernel, ne, nt),
        out_shape=jax.ShapeDtypeStruct((T, width), BF16),
        in_specs=[hbm, vmem, vmem, vmem] + [hbm] * 6,
        out_specs=vmem,
        scratch_shapes=[
            pltpu.VMEM((ne, T, Ds), BF16),
            pltpu.VMEM((ne, T, Ds), BF16),
            pltpu.VMEM((ne, Ds, F), BF16),
            pltpu.VMEM((ne, Ds, F), BF16),
            pltpu.VMEM((ne, F, Ds), BF16),
            pltpu.VMEM((D, FE), BF16),
            pltpu.VMEM((D, FE), BF16),
            pltpu.VMEM((FE, D), BF16),
            pltpu.VMEM((ne, rows, D), BF16),
            pltpu.VMEM((ne, rows, D), BF16),
            pltpu.VMEM((ne, rows, D), BF16),
            pltpu.VMEM((ne, rows, D), BF16),
            pltpu.VMEM((T, F), F32),
            pltpu.VMEM((T, F), F32),
            pltpu.VMEM((T, F), BF16),
            pltpu.VMEM((ne * rows, FE), F32),
            pltpu.VMEM((ne * rows, FE), F32),
            pltpu.VMEM((ne * rows, FE), BF16),
            pltpu.VMEM((others * spt, T, Ds), BF16),
            pltpu.VMEM((others * spt, T, Ds), BF16),
            pltpu.VMEM((spt, T, Ds), BF16),
            dma((2, steps)), dma((2, steps)), dma((2, steps)), dma((2, steps)),
            dma((others, spt)), dma((others, spt)),
            dma((steps,)), dma((steps,)), dma((steps,)), dma((steps,)),
            dma((others * spt,)), dma((others * spt,)),
            dma((spt,)), dma((spt,)),
            dma((3,)), dma((3,)), dma((spt,)),
            pltpu.SemaphoreType.REGULAR,
        ],
        compiler_params=pltpu.CompilerParams(
            collective_id=0, has_side_effects=True, vmem_limit_bytes=60 * 1024 * 1024
        ),
    )(
        tokens.reshape(T, width), norm_gain[0].reshape(ne, 1, Ds), picker, combine,
        shared_gate[0], shared_up[0], shared_down[0],
        expert_gate[0, 0], expert_up[0, 0], expert_down[0, 0],
    )
    return out.reshape(1, batches, block, width)


def solution(mesh):
    in_specs = (
        P(None, "expert", "tensor"),
        P("pipe", None),
        P("pipe", "expert", "tensor"),
        P("pipe", "expert", "tensor"),
        P("pipe", "tensor", "expert"),
        P("pipe", "expert", None, "tensor"),
        P("pipe", "expert", None, "tensor"),
        P("pipe", "expert", "tensor", None),
        P("pipe", None, "expert", None),
        P("pipe", None, "expert", None),
        P("pipe", None, "expert", None),
    )
    out_specs = P("pipe", None, "expert", "tensor")
    return jax.shard_map(
        per_device, mesh=mesh, in_specs=in_specs, out_specs=out_specs, check_vma=False
    )
```

time: 465 us -> 197 us (0.42)
  waiting for transfers between devices: 257 us -> 0 us
  Pallas kernels: 0 us -> 189 us
  blocking collectives: 78.6 us -> 0 us
  matrix products: 70.4 us -> 0 us
  starting transfers between devices: 30.1 us -> 0 us
  between operations: 13.7 us -> 0.04 us
  other arithmetic: 7.68 us -> 2.75 us
    pallas_call x0 -> x1, Pallas kernels: none -> 189 us  [per_device(): pl.pallas_call(functools.partial(layer_kernel, ne, nt), out_shape=jax.Sha...]
    all_gather x3 -> x0, waiting for transfers between devices: 170 us -> none  [the longest x1 74.9 us: per_device(): lax.all_gather(shared_down[0], 'expert', axis=1, tiled=True)]
    dot_general x24 -> x0, matrix products: 70.4 us -> none  [the longest x20 68.3 us: product(): return jnp.dot(left, right, preferred_element_type=jnp.float32)]
    reduce_scatter x4 -> x0, waiting for transfers between devices: 57.9 us -> none  [per_device(): lax.psum_scatter((partial_value + routed).astype(jnp.bfloat16), 'tensor',...]
    all_to_all x4 -> x0, blocking collectives: 51.2 us -> none  [per_device(): lax.all_to_all(outgoing, 'expert', split_axis=0, concat_axis=0, tiled=True)]
    all_gather x4 -> x0, blocking collectives: 27.4 us -> none  [per_device(): full_rows = lax.all_gather(current, 'tensor', axis=1, tiled=True)]
    all_to_all x4 -> x0, starting transfers between devices: 26.1 us -> none  [per_device(): lax.all_to_all(outcome, 'expert', split_axis=0, concat_axis=0, tiled=True)]
    all_to_all x4 -> x0, waiting for transfers between devices: 20.8 us -> none  [per_device(): lax.all_to_all(outcome, 'expert', split_axis=0, concat_axis=0, tiled=True)]
  transfers between devices with their start and end apart: 14 -> 0, of which waited for: 14 -> 0; matrix products, arithmetic and copies ran while one was open for 5% -> 0% of each run, Pallas kernels for 0% -> 0%
where the time goes in v1:
time: 197 us; the launch traced here: 196 us
  Pallas kernels  189 us (96%)
  local copies, waits for them, and re-layouts  4.68 us (2%)
  other arithmetic  2.75 us (1%)
    pallas_call x1, Pallas kernels, per_device(): pl.pallas_call(functools.partial(layer_kernel, ne, nt), out_shape=jax.Sha...  189 us

profile of v1, /device:TPU:13, one launch (start us, length us, event | category | flops | bytes accessed | tf_op | source)
XLA Modules:
  0.0 196.3 jit_solution(18094531062970568646)
XLA Ops:
  0.0 0.1 add.23
  0.1 0.1 add.24
  0.2 0.7 broadcast_compare_fusion
  0.9 0.1 lt.15
  1.0 0.7 broadcast_multiply_fusion
  1.7 0.1 mul.23
  1.8 0.7 copy.26
  2.5 0.1 squeeze.22
  2.6 0.1 copy.28
  2.7 0.3 fusion
  3.0 0.7 copy.29
  3.7 0.8 copy.32
  4.5 1.0 select_reduce_fusion.combine
  5.5 188.8 %shard_map.109 = bf16[144,2048]{1,0:T(8,128)(2,1)} custom-call(bf16[144,2048]{1,0:T(8,128)(2,1)} %bitcast.21, f32[8,1,512]{2,1,0:T(1,128)} %bitcast.27, bf16[128,144]{1,0:T(8,128)(2,1)} %bitcast.26, f32[144,128]{1,0:T(8,128)} %select_reduce_fusion.combine, bf16[512,512]{1,0:T(8,128)(2,1)} %bitcast.22, bf16[512,512]{1,0:T(8,128)(2,1)} %bitcast.23, ...), custom_call_target="tpu_custom_call" | custom-call | tf_op jit(solution)/shard_map/pallas_call | solution.py:305
  194.4 1.9 copy.35
  (5 shorter events, 0.0 us)

commit v2 on v1

--- a/solution.py
+++ b/solution.py
@@ -8,6 +8,11 @@
 from jax.sharding import PartitionSpec as P
 
 CAP = 3
+GATE_PIECES = 2
+DOWN_PIECES = 1
+EARLY = (0.15, 0.24, 0.45)
+EXPERT_END = 0.88
+LAST = 0.9
 MESH = pl.DeviceIdType.MESH
 F32 = jnp.float32
 BF16 = jnp.bfloat16
@@ -26,9 +31,9 @@
     x_hbm, gain, picker, combine, sg_hbm, su_hbm, sd_hbm, eg_hbm, eu_hbm, ed_hbm,
     out,
     xs, xn, sg, su, sd, eg, eu, ed,
-    outg, arr, outc, ret, g_acc, u_acc, hid, eg_acc, eu_acc, ehid, y, rs, res,
+    outg, arr, outc, ret, hy, hr, g_acc, u_acc, hid, eg_acc, eu_acc, ehid, y, rs, res,
     w_send, w_recv, d_send, d_recv, x_send, x_recv, a_send, a_recv, b_send, b_recv,
-    r_send, r_recv, p_send, p_recv, own_sem, exp_sem, x_sem, go_sem,
+    f_send, f_recv, h_send, h_recv, r_send, r_recv, p_send, p_recv, own_sem, exp_sem, x_sem, go_sem,
 ):
     pipe = lax.axis_index("pipe")
     ten = lax.axis_index("tensor")
@@ -89,28 +94,33 @@
 
     right, left = at(pos + 1), at(pos - 1)
 
-    def gate_copy(s):
-        block = sg.at[at(pos - s)]
-        return remote(block, block, w_send.at[0, s], w_recv.at[0, s], expert=right)
-
-    def up_copy(s):
-        block = su.at[at(pos + s)]
-        return remote(block, block, w_send.at[1, s], w_recv.at[1, s], expert=left)
-
-    def down_a(s):
-        block = sd.at[at(pos - s), pl.ds(0, half)]
-        return remote(block, block, d_send.at[0, s], d_recv.at[0, s], expert=right)
-
-    def down_b(s):
-        block = sd.at[at(pos + s), pl.ds(half, half)]
-        return remote(block, block, d_send.at[1, s], d_recv.at[1, s], expert=left)
-
-    def ring(s):
-        for group in ((gate_copy, up_copy), (down_a, down_b)):
-            for make in group:
-                make(s).wait_recv()
-                if s + 1 < ne - 1:
-                    make(s + 1).start()
+    gate_rows, down_rows = Ds // GATE_PIECES, half // DOWN_PIECES
+
+    def gate_copy(s, p):
+        block = sg.at[at(pos - s), pl.ds(p * gate_rows, gate_rows)]
+        return remote(block, block, w_send.at[0, s, p], w_recv.at[0, s, p], expert=right)
+
+    def up_copy(s, p):
+        block = su.at[at(pos + s), pl.ds(p * gate_rows, gate_rows)]
+        return remote(block, block, w_send.at[1, s, p], w_recv.at[1, s, p], expert=left)
+
+    def down_a(s, p):
+        block = sd.at[at(pos - s), pl.ds(p * down_rows, down_rows)]
+        return remote(block, block, d_send.at[0, s, p], d_recv.at[0, s, p], expert=right)
+
+    def down_b(s, p):
+        block = sd.at[at(pos + s), pl.ds(half + p * down_rows, down_rows)]
+        return remote(block, block, d_send.at[1, s, p], d_recv.at[1, s, p], expert=left)
+
+    pieces = [(make, p) for p in range(GATE_PIECES) for make in (gate_copy, up_copy)]
+    pieces += [(make, p) for p in range(DOWN_PIECES) for make in (down_a, down_b)]
+    events = [(s, make, p) for s in range(ne - 1) for make, p in pieces]
+
+    def ring(begin, end):
+        for s, make, p in events[int(begin * len(events)):int(end * len(events))]:
+            make(s, p).wait_recv()
+            if s + 1 < ne - 1:
+                make(s + 1, p).start()
 
     @pl.when(pipe == 1)
     def _():
@@ -118,8 +128,8 @@
 
     for copy in own:
         copy.wait()
-    for make in (gate_copy, up_copy, down_a, down_b):
-        make(0).start()
+    for make, p in pieces:
+        make(0, p).start()
 
     @pl.when(pipe == 0)
     def _():
@@ -128,6 +138,7 @@
 
     @pl.when(pipe == 1)
     def _():
+        ring(0.0, EARLY[-1])
         for i in range(spt):
             block = xs.at[base + i]
             remote(block, block, p_send.at[i], p_recv.at[i], pipe=1 - pipe).wait_recv()
@@ -139,7 +150,11 @@
     for k in range(1, nt):
         for i in range(spt):
             x_copy(k, i).start()
-    ring(0)
+
+    @pl.when(pipe == 0)
+    def _():
+        ring(0.0, EARLY[0])
+
     for k in range(1, nt):
         for i in range(spt):
             x_copy(k, i).wait_recv()
@@ -151,18 +166,28 @@
     total = lax.fori_loop(0, ne, squares, jnp.zeros((T, 1), F32))
     inverse = lax.rsqrt(total / (ne * Ds) + 1e-06)
 
-    def normalise(j, carry):
+    def column(i):
+        return pl.ds(pl.multiple_of(i * Ds, 128), Ds)
+
+    def normed(j):
         v = (xs[j].astype(F32) * inverse * gain[j]).astype(BF16)
         xn[j] = v
-        sent = product(picker[...], v).astype(BF16).reshape(ne, rows, Ds)
-        outg[:, :, pl.ds(pl.multiple_of(j * Ds, 128), Ds)] = sent
+        return v
+
+    def normalise_own(i, carry):
+        sent = product(picker[...], normed(base + i)).astype(BF16)
+        outg[:, :, column(i)] = sent.reshape(ne, rows, Ds)
         return carry
 
-    lax.fori_loop(0, ne, normalise, 0)
+    lax.fori_loop(0, spt, normalise_own, 0)
 
     def dispatch(k):
         to = (me + k) % ne
-        return remote(outg.at[to], arr.at[me], a_send.at[k - 1], a_recv.at[k - 1], expert=to)
+        return remote(outg.at[to], arr.at[ten, me], a_send.at[k - 1], a_recv.at[k - 1], expert=to)
+
+    def spread(q, k):
+        block = arr.at[ten, (me + ne - k) % ne]
+        return remote(block, block, f_send.at[q - 1, k], f_recv.at[q - 1, k], tensor=(ten + q) % nt)
 
     def give_back(k):
         to = (me + k) % ne
@@ -170,8 +195,19 @@
 
     for k in range(1, ne):
         dispatch(k).start()
-    arr[me] = outg[me]
-
+    arr[ten, me] = outg[me]
+    for q in range(1, nt):
+        spread(q, 0).start()
+
+    @pl.when(pipe == 0)
+    def _():
+        ring(EARLY[0], EARLY[1])
+
+    def normalise_others(j, carry):
+        normed((base + spt + j) % ne)
+        return carry
+
+    lax.fori_loop(0, ne - spt, normalise_others, 0)
     g_acc[...] = product(xn[me], sg[me])
     u_acc[...] = product(xn[me], su[me])
 
@@ -180,72 +216,104 @@
         g_acc[...] += product(xn[a], sg[a])
         u_acc[...] += product(xn[b], su[b])
 
-    ring(1)
-    ring(2)
+    @pl.when(pipe == 0)
+    def _():
+        ring(EARLY[1], EARLY[2])
+
     for copy in experts:
         copy.wait()
     for k in range(1, ne):
         dispatch(k).wait_recv()
+        for q in range(1, nt):
+            spread(q, k).start()
+    ticks = [EARLY[2]]
+
+    def tick():
+        later = ticks[0] + (EXPERT_END - EARLY[2]) / (4 * ne)
+        ring(ticks[0], later)
+        ticks[0] = later
+
     eg_acc[...] = jnp.zeros_like(eg_acc)
     eu_acc[...] = jnp.zeros_like(eu_acc)
 
-    def expert_in(j, carry):
-        depth = pl.ds(pl.multiple_of(j * Ds, 128), Ds)
-        v = arr[:, :, depth].reshape(ne * rows, Ds)
-        eg_acc[...] += product(v, eg[depth, :])
-        eu_acc[...] += product(v, eu[depth, :])
-        return carry
-
-    lax.fori_loop(0, ne // 2, expert_in, 0)
-    ring(3)
-    lax.fori_loop(ne // 2, ne, expert_in, 0)
+    def expert_in(group):
+        for i in range(spt):
+            depth = pl.ds(pl.multiple_of(group * (spt * Ds) + i * Ds, 128), Ds)
+            v = arr[group, :, :, i * Ds:(i + 1) * Ds].reshape(ne * rows, Ds)
+            eg_acc[...] += product(v, eg[depth, :])
+            tick()
+            eu_acc[...] += product(v, eu[depth, :])
+            tick()
+
+    expert_in(ten)
+    for q in range(1, nt):
+        for k in range(ne):
+            spread(q, k).wait_recv()
+        expert_in((ten + q) % nt)
     ehid[...] = (silu(eg_acc[...]) * eu_acc[...]).astype(BF16)
 
-    def expert_out(j, carry):
-        width = pl.ds(pl.multiple_of(j * Ds, 128), Ds)
-        outc[:, :, width] = product(ehid[...], ed[:, width]).astype(BF16).reshape(ne, rows, Ds)
-        return carry
-
-    lax.fori_loop(0, ne, expert_out, 0)
+    def h_copy(q, i):
+        slot = (q - 1) * spt + i
+        return remote(hy.at[slot], hr.at[slot], h_send.at[slot], h_recv.at[slot], tensor=(ten + q) % nt)
+
+    def expert_out(group, i):
+        return product(ehid[...], ed[:, pl.ds(pl.multiple_of(group * (spt * Ds) + i * Ds, 128), Ds)])
+
+    for q in range(1, nt):
+        for i in range(spt):
+            hy[(q - 1) * spt + i] = expert_out((ten + q) % nt, i).astype(BF16)
+            h_copy(q, i).start()
+            tick()
+            tick()
+    for i in range(spt):
+        value = expert_out(ten, i)
+        for q in range(1, nt):
+            h_copy(q, i).wait_recv()
+            value += hr[(q - 1) * spt + i].astype(F32)
+        outc[:, :, i * Ds:(i + 1) * Ds] = value.astype(BF16).reshape(ne, rows, Ds)
+        tick()
+        tick()
     for k in range(1, ne):
         give_back(k).start()
     ret[me] = outc[me]
-    for s in range(4, ne - 1):
-        ring(s)
-        if s < ne - 2:
-            if s == 4:
-                for q in range(4):
-                    shared(q)
-            shared(s)
-
-    @pl.when(pipe == 0)
-    def _():
-        pl.semaphore_signal(go_sem, inc=1, device_id={"pipe": 1 - pipe}, device_id_type=MESH)
-
+    held = ticks[0]
+    for s in range(ne - 2):
+        later = max(held, min(held + (LAST - held) * (s + 1) / (ne - 3), (s + 2) / (ne - 1), 1.0))
+        if s == ne - 3:
+            @pl.when(pipe == 0)
+            def _():
+                pl.semaphore_signal(go_sem, inc=1, device_id={"pipe": 1 - pipe}, device_id_type=MESH)
+
+            later = 1.0
+        ring(held, max(held, (s + 1) / (ne - 1)))
+        held = max(held, (s + 1) / (ne - 1))
+        shared(s)
+        ring(held, max(held, later))
+        held = max(held, later)
     shared(ne - 2)
     hid[...] = (silu(g_acc[...]) * u_acc[...]).astype(BF16)
+
+    def terms(j):
+        return product(hid[...], sd[j])
+
+    def r_copy(k, i):
+        to = (ten + k) % nt
+        slot = (k - 1) * spt + i
+        return remote(y.at[slot], rs.at[slot], r_send.at[slot], r_recv.at[slot], tensor=to)
+
+    for k in range(1, nt):
+        for i in range(spt):
+            y[(k - 1) * spt + i] = terms(((ten + k) % nt) * spt + i).astype(BF16)
+            r_copy(k, i).start()
+
     for k in range(1, ne):
         give_back(k).wait_recv()
     weights = combine[...]
     high = weights.astype(BF16)
     low = (weights - high.astype(F32)).astype(BF16)
-
-    def terms(j):
-        v = ret[:, :, pl.ds(pl.multiple_of(j * Ds, 128), Ds)].reshape(ne * rows, Ds)
-        return product(hid[...], sd[j]) + (product(high, v) + product(low, v))
-
-    def r_copy(k, i):
-        to = (ten + k) % nt
-        slot = (k - 1) * spt + i
-        return remote(y.at[slot], rs.at[slot], r_send.at[slot], r_recv.at[slot], tensor=to)
-
-    for k in range(1, nt):
-        for i in range(spt):
-            y[(k - 1) * spt + i] = terms(((ten + k) % nt) * spt + i).astype(BF16)
-            r_copy(k, i).start()
-
     for i in range(spt):
-        value = xs[base + i].astype(F32) + terms(base + i)
+        v = ret[:, :, i * Ds:(i + 1) * Ds].reshape(ne * rows, Ds)
+        value = xs[base + i].astype(F32) + terms(base + i) + (product(high, v) + product(low, v))
         for k in range(1, nt):
             r_copy(k, i).wait_recv()
             value += rs[(k - 1) * spt + i].astype(F32)
@@ -258,8 +326,8 @@
             remote(res.at[i], xs.at[base + i], p_send.at[i], p_recv.at[i], pipe=1 - pipe).start()
 
     for s in range(ne - 1):
-        for make in (gate_copy, up_copy, down_a, down_b):
-            make(s).wait_send()
+        for make, p in pieces:
+            make(s, p).wait_send()
     for k in range(1, ne):
         dispatch(k).wait_send()
         give_back(k).wait_send()
@@ -267,6 +335,9 @@
         for i in range(spt):
             x_copy(k, i).wait_send()
             r_copy(k, i).wait_send()
+            h_copy(k, i).wait_send()
+        for i in range(ne):
+            spread(k, i).wait_send()
 
     @pl.when(pipe == 0)
     def _():
@@ -316,10 +387,12 @@
             pltpu.VMEM((D, FE), BF16),
             pltpu.VMEM((D, FE), BF16),
             pltpu.VMEM((FE, D), BF16),
-            pltpu.VMEM((ne, rows, D), BF16),
-            pltpu.VMEM((ne, rows, D), BF16),
-            pltpu.VMEM((ne, rows, D), BF16),
-            pltpu.VMEM((ne, rows, D), BF16),
+            pltpu.VMEM((ne, rows, width), BF16),
+            pltpu.VMEM((nt, ne, rows, width), BF16),
+            pltpu.VMEM((ne, rows, width), BF16),
+            pltpu.VMEM((ne, rows, width), BF16),
+            pltpu.VMEM((others * spt, ne * rows, Ds), BF16),
+            pltpu.VMEM((others * spt, ne * rows, Ds), BF16),
             pltpu.VMEM((T, F), F32),
             pltpu.VMEM((T, F), F32),
             pltpu.VMEM((T, F), BF16),
@@ -329,9 +402,12 @@
             pltpu.VMEM((others * spt, T, Ds), BF16),
             pltpu.VMEM((others * spt, T, Ds), BF16),
             pltpu.VMEM((spt, T, Ds), BF16),
-            dma((2, steps)), dma((2, steps)), dma((2, steps)), dma((2, steps)),
+            dma((2, steps, GATE_PIECES)), dma((2, steps, GATE_PIECES)),
+            dma((2, steps, DOWN_PIECES)), dma((2, steps, DOWN_PIECES)),
             dma((others, spt)), dma((others, spt)),
             dma((steps,)), dma((steps,)), dma((steps,)), dma((steps,)),
+            dma((others, ne)), dma((others, ne)),
+            dma((others * spt,)), dma((others * spt,)),
             dma((others * spt,)), dma((others * spt,)),
             dma((spt,)), dma((spt,)),
             dma((3,)), dma((3,)), dma((spt,)),

time: 197 us -> 166 us (0.84)
  Pallas kernels: 189 us -> 156 us
    pallas_call x1, Pallas kernels: 189 us -> 156 us  [per_device(): pl.pallas_call(functools.partial(layer_kernel, ne, nt), out_shape=jax.Sha...]
where the time goes in v2:
time: 166 us; the launch traced here: 163 us
  Pallas kernels  156 us (94%)
  local copies, waits for them, and re-layouts  4.68 us (3%)
  other arithmetic  2.75 us (2%)
    pallas_call x1, Pallas kernels, per_device(): pl.pallas_call(functools.partial(layer_kernel, ne, nt), out_shape=jax.Sha...  156 us

profile of v2, /device:TPU:13, one launch (start us, length us, event | category | flops | bytes accessed | tf_op | source)
XLA Modules:
  0.0 163.4 jit_solution(9441655410457279137)
XLA Ops:
  0.0 0.1 add.23
  0.1 0.1 add.24
  0.2 0.7 broadcast_compare_fusion
  0.9 0.1 lt.15
  1.0 0.7 broadcast_multiply_fusion
  1.7 0.1 mul.23
  1.8 0.7 copy.26
  2.5 0.1 squeeze.22
  2.6 0.1 copy.28
  2.7 0.3 fusion
  3.0 0.7 copy.29
  3.7 0.8 copy.32
  4.5 1.0 select_reduce_fusion.combine
  5.5 155.9 %shard_map.109 = bf16[144,2048]{1,0:T(8,128)(2,1)} custom-call(bf16[144,2048]{1,0:T(8,128)(2,1)} %bitcast.21, f32[8,1,512]{2,1,0:T(1,128)} %bitcast.27, bf16[128,144]{1,0:T(8,128)(2,1)} %bitcast.26, f32[144,128]{1,0:T(8,128)} %select_reduce_fusion.combine, bf16[512,512]{1,0:T(8,128)(2,1)} %bitcast.22, bf16[512,512]{1,0:T(8,128)(2,1)} %bitcast.23, ...), custom_call_target="tpu_custom_call" | custom-call | tf_op jit(solution)/shard_map/pallas_call | solution.py:376
  161.5 1.9 %copy.35 = bf16[1,3,48,2048]{3,2,1,0:T(8,128)(2,1)} copy(bf16[1,3,48,2048]{3,2,1,0:T(8,128)(2,1)} %bitcast.20) | data formatting | bytes 1179648
  (5 shorter events, 0.0 us)
